TPU v7x, 128 devices: a whole 4x4x4 slice. The times are simulated.
128 devices in a mesh: dp: 32 (over x, z, core), tensor: 4 (over y).
Axes of the slice: x: 4, y: 4, z: 4, core: 2. Of those that a mesh axis runs over, the one named last changes fastest.
Arguments:
- tokens: bfloat16 [16384, 4096], P(('dp', 'tensor')), may hold values from -6 to 6
- norm_gain: float32 [4096], replicated, may hold values from 0.1 to 1.9
- w_query: bfloat16 [4096, 2048], P(None, 'tensor'), may hold values from -2 to 2
- key_weight: bfloat16 [4096, 512], P(None, 'tensor'), may hold values from -0.09375 to 0.09375
- value_weight: bfloat16 [4096, 512], P(None, 'tensor'), may hold values from -0.09375 to 0.09375
- w_out: bfloat16 [2048, 4096], P('tensor'), may hold values from -0.125 to 0.125
- lengths: int32 [16], replicated, may hold values from 1 to 8704, 16384 in all
Outputs:
- layer_out: bfloat16 [16384, 4096], P(('dp', 'tensor'))
Inputs may be any that keep to these rules, and one draw needn't show every extreme that they name: The lengths sum to 16384, and some document has exactly 8704 tokens.
All inputs are finite; a program needn't handle non-finite values.
Results may differ from a plain program's by a relative error of at most 0.0095.
The roundings to bfloat16 on the way count: a program that leaves them out, or rounds other values in their place, can miss the bound.
Values may be sent and summed in bfloat16 or wider, within the bound.
No kernel may reach another device: no remote copies, remote signals or barrier semaphores. Data moves between devices by JAX's collectives and lax.ppermute only.
A program may use at most 128 MiB of HBM per device.

v0:
```python
import jax
import jax.numpy as jnp
from jax import lax
from jax.sharding import PartitionSpec as P

HEAD_SIZE = 128
epsilon = 1e-05
rope_base = 500000.0
masked = -1e30
initial_peak = -1e29


def in_one_piece(arrays, axis, dim, along):
    ends, at = ([], 0)
    for a in arrays[:-1]:
        at += a.shape[along]
        ends.append(at)
    both = jnp.concatenate(arrays, axis=along)
    return tuple(jnp.split(lax.all_gather(both, axis, axis=dim, tiled=True), ends, axis=along))


def doc_starts(lengths, positions):
    doc_ends = jnp.cumsum(lengths)
    closed = (doc_ends[None, :] <= positions[:, None]).astype(jnp.int32)
    return jnp.sum(closed * lengths[None, :], axis=1)


def rotate(vectors, offsets):
    half_width = vectors.shape[-1] // 2
    exponent = jnp.arange(half_width, dtype=jnp.float32) * (-2.0 / vectors.shape[-1])
    frequency = rope_base**exponent
    angles = offsets.astype(jnp.float32)[:, None] * frequency[None, :]
    cos_part = jnp.cos(angles)[:, None, :]
    sin_part = jnp.sin(angles)[:, None, :]
    leading = vectors[..., :half_width]
    trailing = vectors[..., half_width:]
    return jnp.concatenate(
        [leading * cos_part - trailing * sin_part, trailing * cos_part + leading * sin_part],
        axis=-1,
    )


def project(tokens, norm_gain, w_query, key_weight, value_weight, positions, starts):
    count = tokens.shape[0]
    wide = tokens.astype(jnp.float32)
    inverse = lax.rsqrt(jnp.mean(wide * wide, axis=1, keepdims=True) + epsilon)
    normed = (wide * inverse * norm_gain[None, :]).astype(jnp.bfloat16)
    offsets = positions - starts
    query_rows = jnp.dot(normed, w_query, preferred_element_type=jnp.float32).reshape(
        count, -1, HEAD_SIZE
    )
    query_rows = rotate(query_rows, offsets).astype(jnp.bfloat16)
    key = jnp.dot(normed, key_weight, preferred_element_type=jnp.float32).reshape(
        count, -1, HEAD_SIZE
    )
    key = rotate(key, offsets).astype(jnp.bfloat16)
    value_rows = jnp.dot(normed, value_weight, preferred_element_type=jnp.float32).astype(
        jnp.bfloat16
    )
    return (query_rows, key.reshape(count, -1), value_rows)


def attend_block(carry, keys, values, first_key, context):
    query_rows, positions, starts = context
    length = keys.shape[0]
    heads = query_rows.shape[1]
    key_pos = first_key + jnp.arange(length, dtype=jnp.int32)
    useful = (first_key + length - 1 >= starts[0]) & (first_key <= positions[-1])
    scale = query_rows.shape[-1] ** (-0.5)

    def compute(state):
        peak, mass, summed = state
        key_view = keys.reshape(length, heads, -1)
        value_view = values.reshape(length, heads, -1)
        scores = (
            jnp.einsum("qkgd,skd->qkgs", query_rows, key_view, preferred_element_type=jnp.float32)
            * scale
        )
        visible = (key_pos[None, :] >= starts[:, None]) & (key_pos[None, :] <= positions[:, None])
        scores = jnp.where(visible[:, None, None, :], scores, masked)
        fresh = jnp.maximum(peak, jnp.max(scores, axis=-1))
        shrink = jnp.exp(peak - fresh)
        probs = jnp.exp(scores - fresh[..., None])
        mass = mass * shrink + jnp.sum(probs, axis=-1)
        update = jnp.einsum(
            "qkgs,skd->qkgd",
            probs.astype(jnp.bfloat16),
            value_view,
            preferred_element_type=jnp.float32,
        )
        summed = summed * shrink[..., None] + update
        return (fresh, mass, summed)

    def unchanged(state):
        return state

    return lax.cond(useful, compute, unchanged, carry)


def fold_keys(carry, pieces, context):
    keys, values = pieces
    width = keys.shape[0]
    size = min(width, 1024)
    whole = width // size

    def one_block(index, state):
        offset = (index * size).astype(jnp.int32)
        key_part = lax.dynamic_slice_in_dim(keys, offset, size, 0)
        value_part = lax.dynamic_slice_in_dim(values, offset, size, 0)
        return attend_block(state, key_part, value_part, offset, context)

    carry = lax.fori_loop(0, whole, one_block, carry)
    return carry


def body(tokens, norm_gain, w_query, key_weight, value_weight, w_out, lengths):
    gathered = lax.all_gather(tokens, "tensor", axis=0, tiled=True)
    count = gathered.shape[0]
    first = lax.axis_index("dp") * count
    positions = first + jnp.arange(count, dtype=jnp.int32)
    starts = doc_starts(lengths, positions)
    query_rows, key, value_rows = project(
        gathered, norm_gain, w_query, key_weight, value_weight, positions, starts
    )
    heads = key.shape[1] // HEAD_SIZE
    query_rows = query_rows.reshape(count, heads, -1, HEAD_SIZE)
    group_count = query_rows.shape[2]
    context = (query_rows, positions, starts)
    initial = (
        jnp.full((count, heads, group_count), initial_peak, jnp.float32),
        jnp.zeros((count, heads, group_count), jnp.float32),
        jnp.zeros((count, heads, group_count, HEAD_SIZE), jnp.float32),
    )
    carry = fold_keys(initial, in_one_piece((key, value_rows), "dp", 0, 1), context)
    peak, mass, summed = carry
    attended = (summed / mass[..., None]).reshape(count, -1).astype(jnp.bfloat16)
    branch = lax.psum_scatter(
        jnp.dot(attended, w_out, preferred_element_type=jnp.float32).astype(jnp.bfloat16),
        "tensor",
        scatter_dimension=0,
        tiled=True,
    ).astype(jnp.float32)
    return (tokens.astype(jnp.float32) + branch).astype(jnp.bfloat16)


def solution(mesh):
    in_specs = (
        P(("dp", "tensor"), None),
        P(),
        P(None, "tensor"),
        P(None, "tensor"),
        P(None, "tensor"),
        P("tensor", None),
        P(),
    )
    out_specs = P(("dp", "tensor"), None)
    return jax.shard_map(body, mesh=mesh, in_specs=in_specs, out_specs=out_specs, check_vma=False)
```

profile of v0, /device:TPU:1, one launch (start us, length us, event | category | flops | bytes accessed | tf_op | source)
XLA Modules:
  0.0 329.1 jit_solution(13975362636619700645)
XLA Ops:
  6.5 0.7 all-gather.3.cloned.1.call-update
  7.3 0.7 copy.19
  8.2 0.7 select_reduce_fusion
  9.0 51.3 %all-gather.3.cloned.1.call-done = bf16[512,4096]{1,0:T(8,128)(2,1)} async-done(((bf16[128,4096]{1,0:T(8,128)(2,1)}), bf16[512,4096]{1,0:T(8,128)(2,1)}) %all-gather.3.cloned.1.call-update) | async-done | bytes 4194320 | tf_op jit(solution)/shard_map/all_gather | solution.py:117
  60.3 3.2 fusion.24
  63.7 1.6 convolution_bitcast_fusion
  65.9 1.6 convolution_convert_fusion.1
  67.5 0.7 pad_maximum_fusion.1
  68.5 1.8 multiply_cosine_fusion
  70.3 5.9 %fusion.39 = f32[512,512]{0,1:T(8,128)S(1)} fusion(bf16[4096,512]{1,0:T(8,128)(2,1)} %param.13, bf16[512,4096]{1,0:T(8,128)(2,1)} %all-gather.3.cloned.1.call-done, f32[4096]{0:T(1024)S(1)} %copy-done.4, f32[512]{0:T(512)S(1)} %add_rsqrt_fusion), kind=kOutput, calls=%fused_computation.61 | convolution fusion | flops 2155872256 | bytes 9455616 | tf_op jit(solution)/shard_map/dot_general | solution.py:49
  76.2 0.9 fusion.44
  77.5 1.4 copy.24
  78.9 1.2 fusion.27
  80.4 47.9 %all-gather.5.cloned.1.call-done = bf16[16384,256]{0,1:T(8,128)(2,1)} async-done(((bf16[512,256]{0,1:T(8,128)(2,1)}), bf16[16384,256]{0,1:T(8,128)(2,1)}) %all-gather.5.cloned.1.call-update) | async-done | bytes 8388624 | tf_op jit(solution)/shard_map/all_gather | solution.py:19
  128.3 5.8 %fusion.43 = (bf16[16384,128]{0,1:T(8,128)(2,1)}, bf16[16384,128]{0,1:T(8,128)(2,1)}) fusion(bf16[16384,256]{0,1:T(8,128)(2,1)} %all-gather.5.cloned.1.call-done), kind=kLoop, calls=%fused_computation.62 | loop fusion | bytes 16777216 | tf_op jit(solution)/shard_map/split | solution.py:19
  134.0 6.4 %copy.22 = bf16[16384,128]{1,0:T(8,128)(2,1)} copy(bf16[16384,128]{0,1:T(8,128)(2,1)} %get-tuple-element.495) | data formatting | bytes 8388608 | tf_op jit(solution)/shard_map/while | solution.py:112
  140.5 51.2 %while.21 = (s32[]{:T(128)}, f32[512,1,4]{0,2,1:T(4,128)S(1)}, f32[512,1,4]{0,2,1:T(4,128)S(1)}, f32[512,1,4,128]{0,3,2,1:T(8,128)S(1)}, s32[512]{0:T(512)S(1)},...) while((s32[]{:T(128)}, f32[512,1,4]{0,2,1:T(4,128)S(1)}, ...), condition=%wide.region_8.9_spmd, body=%wide.region_3.8_spmd.sunk | while | flops 1098914816 | bytes 30560620 | solution.py:112
  141.8 0.6 slice.63
  143.2 8.5 %conditional.2 = ((f32[512,1,4]{0,2,1:T(4,128)S(1)}, f32[512,1,4]{0,2,1:T(4,128)S(1)}, f32[512,1,4,128]{0,3,2,1:T(8,128)S(1)})) conditional(s32[]{:T(128)} %convert_element_type.108, (f32[512,1,4]{0,2,1:T(4,128)S(1)}, f32[512,1,4]{0,2,1:T(4,128)S(1)}, f32[512,1,4,128]{0,3,2,1:T(8,128)S(1)}) %tuple.77, (s32[]{:T(128)}, s32[1024]{0:T(1024)S(1)}, ...), branch_computations={%region_4.4_spmd, %region_5.7_spmd} | conditional | flops 1098914816 | bytes 30556238 | solution.py:97
  143.7 2.5 fusion.2
  146.2 3.5 %fusion.10 = f32[512,1,4,128]{0,3,2,1:T(8,128)S(1)} fusion(f32[1024,512,4]{1,0,2:T(8,128)S(1)} %get-tuple-element.493, f32[512,4]{0,1:T(4,128)S(1)} %bitcast.76, pred[512,1024]{0,1:T(8,128)(4,1)S(1)} %compare_and_fusion, f32[512,1,4,128]{0,3,2,1:T(8,128)S(1)} %get-tuple-element.426, f32[512,4]{0,1:T(4,128)S(1)} %get-tuple-element.490, ...), kind=kOutput, calls=%fused_computation.10 | convolution fusion | flops 545783808 | bytes 11288580 | tf_op jit(solution)/shard_map/while/body/eval_jaxpr/cond/branch_1_fun/qkgs,skd->qkgd/dot_general | solution.py:85
  149.8 1.8 fusion.1
  152.9 0.6 slice.63
  155.6 0.6 slice.63
  160.9 0.6 slice.63
  163.5 0.6 slice.63
  166.2 0.6 slice.63
  168.9 0.6 slice.63
  174.2 0.6 slice.63
  191.8 6.5 %convolution_convert_fusion = bf16[512,4096]{1,0:T(8,128)(2,1)} fusion(bf16[512,512]{0,1:T(8,128)(2,1)S(1)} %bitcast.78, bf16[512,4096]{1,0:T(8,128)(2,1)} %param.16), kind=kOutput, calls=%fused_computation.31 | convolution fusion | flops 2149580800 | bytes 8912896 | tf_op jit(solution)/shard_map/dot_general | solution.py:138
  198.4 121.8 %reduce-scatter.2.cloned.1.call-done = bf16[128,4096]{1,0:T(8,128)(2,1)} async-done(((bf16[512,4096]{1,0:T(8,128)(2,1)}), bf16[128,4096]{1,0:T(8,128)(2,1)}) %reduce-scatter.2.cloned.1.call-update) | async-done | bytes 1048592 | tf_op jit(solution)/shard_map/reduce_scatter | solution.py:137
  320.1 2.4 add_convert_fusion
  (88 shorter events, 17.3 us)
Async XLA Ops:
  6.5 57.0 %copy-start = (bf16[4096,128]{1,0:T(8,128)(2,1)S(1)}, bf16[4096,128]{1,0:T(8,128)(2,1)}, u32[]{:S(2)}) copy-start(bf16[4096,128]{1,0:T(8,128)(2,1)} %param.14) | copy-start | bytes 3145732
  6.5 57.0 %copy-start.4 = (f32[4096]{0:T(1024)S(1)}, f32[4096]{0:T(1024)}, u32[]{:S(2)}) copy-start(f32[4096]{0:T(1024)} %param.12) | copy-start | bytes 49156
  6.5 53.7 %all-gather.3.cloned.1.call-start = ((), (), s32[]{:S(2)}) async-start(), calls=%async_computation.1 | async-start | bytes 5242880 | tf_op jit(solution)/shard_map/all_gather | solution.py:117
  7.3 121.0 %all-gather.5.cloned.1.call-start = ((), (), s32[]{:S(2)}) async-start(), calls=%async_computation.2 | async-start | bytes 8650752 | tf_op jit(solution)/shard_map/all_gather | solution.py:19
  60.3 3.4 %copy-start.2 = (bf16[512,4096]{1,0:T(8,128)(2,1)S(1)}, bf16[512,4096]{1,0:T(8,128)(2,1)}, u32[]{:S(2)}) copy-start(bf16[512,4096]{1,0:T(8,128)(2,1)} %all-gather.3.cloned.1.call-done) | copy-start | bytes 12582916
  63.7 2.2 copy-start.3
  68.3 251.8 %reduce-scatter.2.cloned.1.call-start = ((), (), s32[]{:S(2)}) async-start(), calls=%async_computation.3 | async-start | bytes 5242880 | tf_op jit(solution)/shard_map/reduce_scatter | solution.py:137
  198.3 121.8 %copy-start.1 = (bf16[128,4096]{1,0:T(8,128)(2,1)S(1)}, bf16[128,4096]{1,0:T(8,128)(2,1)}, u32[]{:S(2)}) copy-start(bf16[128,4096]{1,0:T(8,128)(2,1)} %param.11) | copy-start | bytes 3145732
Sparse Core Ops, SparseCore 0:
  9.0 51.2 all-gather.2
  68.4 59.7 all-gather.4
  198.5 121.6 reduce-scatter.1
where the time goes:
time: 330 us; the launch traced here: 329 us
  waiting for transfers between devices  222 us (67%)
  local copies, waits for them, and re-layouts  35.5 us (11%)
  loops' own time  23.1 us (7%)
  matrix products  21.7 us (7%)
  other arithmetic  13.7 us (4%)
  between operations  13.2 us (4%)
    reduce_scatter x1, waiting for transfers between devices, body(): lax.psum_scatter(jnp.dot(attended, w_out, preferred_element_type=jnp.floa...  122 us
    all_gather x1, waiting for transfers between devices, body(): gathered = lax.all_gather(tokens, 'tensor', axis=0, tiled=True)  51.3 us
    all_gather x1, waiting for transfers between devices, in_one_piece(): lax.all_gather(both, axis, axis=dim, tiled=True)  47.9 us
    another operation x1, loops' own time, fold_keys(): carry = lax.fori_loop(0, whole, one_block, carry)  22.8 us
    slice x16, local copies, waits for them, and re-layouts, attend_block(): positions[-1]  10.4 us
    slice x16, local copies, waits for them, and re-layouts, attend_block(): starts[0]  9.25 us
  transfers between devices with their start and end apart: 3, of which 3 were waited for; matrix products, arithmetic and copies ran while one was open for 4% of the time, Pallas kernels for 0%

commit v1 on v0

--- a/solution.py
+++ b/solution.py
@@ -8,6 +8,10 @@
 rope_base = 500000.0
 masked = -1e30
 initial_peak = -1e29
+produce_the_files = lambda patch, mesh_dim: jnp.concatenate(
+    jax.lax.all_to_all(jnp.stack([patch] * jax.lax.axis_size(mesh_dim), axis=0), mesh_dim, 0, 0),
+    axis=0,
+)
 
 
 def in_one_piece(arrays, axis, dim, along):
@@ -114,7 +118,7 @@
 
 
 def body(tokens, norm_gain, w_query, key_weight, value_weight, w_out, lengths):
-    gathered = lax.all_gather(tokens, "tensor", axis=0, tiled=True)
+    gathered = produce_the_files(tokens, "tensor")
     count = gathered.shape[0]
     first = lax.axis_index("dp") * count
     positions = first + jnp.arange(count, dtype=jnp.int32)

time: 330 us -> 336 us (1.018)
  local copies, waits for them, and re-layouts: 35.5 us -> 41.4 us
  starting transfers between devices: 0.26 us -> 5.36 us
  waiting for transfers between devices: 222 us -> 217 us
  other arithmetic: 13.7 us -> 18.1 us
  matrix products: 21.7 us -> 18.1 us
    all_gather x1 -> x0, waiting for transfers between devices: 51.3 us -> none  [body(): gathered = lax.all_gather(tokens, 'tensor', axis=0, tiled=True)]
    all_to_all x0 -> x1, waiting for transfers between devices: none -> 48.5 us  [jax.lax.all_to_all(jnp.stack([patch] * jax.lax.axis_size(mesh_dim), axis=...]
    convert_element_type x0 -> x2, other arithmetic: none -> 7.8 us  [project(): normed = (wide * inverse * norm_gain[None, :]).astype(jnp.bfloat16)]
    dot_general x0 -> x1, local copies, waits for them, and re-layouts: none -> 6.41 us  [project(): jnp.dot(normed, w_query, preferred_element_type=jnp.float32)]
    all_to_all x0 -> x1, starting transfers between devices: none -> 5.13 us  [jax.lax.all_to_all(jnp.stack([patch] * jax.lax.axis_size(mesh_dim), axis=...]
    dot_general x1, matrix products: 5.92 us -> 2.36 us  [project(): jnp.dot(normed, w_query, preferred_element_type=jnp.float32)]
where the time goes in v1:
time: 336 us; the launch traced here: 334 us
  waiting for transfers between devices  217 us (65%)
  local copies, waits for them, and re-layouts  41.4 us (12%)
  loops' own time  20.8 us (6%)
  other arithmetic  18.1 us (5%)
  matrix products  18.1 us (5%)
  between operations  13.6 us (4%)
  starting transfers between devices  5.36 us (2%)
    reduce_scatter x1, waiting for transfers between devices, body(): lax.psum_scatter(jnp.dot(attended, w_out, preferred_element_type=jnp.floa...  122 us
    all_to_all x1, waiting for transfers between devices, jax.lax.all_to_all(jnp.stack([patch] * jax.lax.axis_size(mesh_dim), axis=...  48.5 us
    all_gather x1, waiting for transfers between devices, in_one_piece(): lax.all_gather(both, axis, axis=dim, tiled=True)  46.8 us
    another operation x1, loops' own time, fold_keys(): carry = lax.fori_loop(0, whole, one_block, carry)  20.5 us
    slice x16, local copies, waits for them, and re-layouts, attend_block(): positions[-1]  9.8 us
    slice x16, local copies, waits for them, and re-layouts, attend_block(): starts[0]  8.68 us
    convert_element_type x2, other arithmetic, project(): normed = (wide * inverse * norm_gain[None, :]).astype(jnp.bfloat16)  7.8 us
  transfers between devices with their start and end apart: 3, of which 3 were waited for; matrix products, arithmetic and copies ran while one was open for 4% of the time, Pallas kernels for 0%

profile of v1, /device:TPU:1, one launch (start us, length us, event | category | flops | bytes accessed | tf_op | source)
XLA Modules:
  0.0 334.4 jit_solution(15973999207493445657)
XLA Ops:
  6.5 3.8 %stack.2 = bf16[4,128,4096]{2,1,0:T(8,128)(2,1)} broadcast(bf16[128,4096]{1,0:T(8,128)(2,1)} %param.11), dimensions={1,2} | broadcast | bytes 5242880 | tf_op jit(solution)/shard_map/stack | solution.py:12
  10.3 5.1 %all-to-all-start = ((bf16[4,128,4096]{2,1,0:T(8,128)(2,1)}), bf16[4,128,4096]{2,1,0:T(8,128)(2,1)}, u32[]{:S(2)}, u32[]{:S(2)}) async-start(bf16[4,128,4096]{2,1,0:T(8,128)(2,1)} %stack.2), calls=%async_computation | async-start | bytes 8388608 | tf_op jit(solution)/shard_map/all_to_all | solution.py:12
  15.8 48.5 %all-to-all-done = bf16[4,128,4096]{2,1,0:T(8,128)(2,1)} async-done(((bf16[4,128,4096]{2,1,0:T(8,128)(2,1)}), bf16[4,128,4096]{2,1,0:T(8,128)(2,1)}, u32[]{:S(2)}, u32[]{:S(2)}) %all-to-all-start) | async-done | bytes 4194336 | tf_op jit(solution)/shard_map/all_to_all | solution.py:12
  64.3 3.1 multiply_reduce_fusion
  67.4 3.8 %fusion.25 = bf16[512,4096]{1,0:T(8,128)(2,1)S(1)} fusion(bf16[4,128,4096]{2,1,0:T(8,128)(2,1)} %all-to-all-done, f32[4096]{0:T(1024)S(1)} %copy-done.5, f32[512]{0:T(512)S(1)} %get-tuple-element.503), kind=kLoop, calls=%fused_computation.28 | loop fusion | flops 8388608 | bytes 8407040 | tf_op jit(solution)/shard_map/convert_element_type | solution.py:51
  71.3 1.5 convolution_convert_fusion.1
  72.8 1.5 convolution_bitcast_fusion
  74.9 0.7 pad_maximum_fusion.1
  75.9 6.4 %copy.24 = bf16[512,4096]{1,0:T(8,128)(2,1)} copy(bf16[512,4096]{0,1:T(8,128)(2,1)} %bitcast.92) | data formatting | bytes 8388608 | tf_op jit(solution)/shard_map/dot_general | solution.py:53
  82.9 4.0 %multiply_convert_fusion = bf16[4,128,4096]{2,1,0:T(8,128)(2,1)S(1)} fusion(bf16[4,128,4096]{2,1,0:T(8,128)(2,1)} %all-to-all-done, f32[4096]{0:T(1024)S(1)} %copy-done.5, f32[4,128]{1,0:T(4,128)S(1)} %get-tuple-element.502), kind=kLoop, calls=%fused_computation.29 | loop fusion | flops 8388608 | bytes 8407040 | tf_op jit(solution)/shard_map/convert_element_type | solution.py:51
  86.9 2.4 fusion.40
  89.7 46.8 %all-gather.2.cloned.1.call-done = bf16[16384,256]{0,1:T(8,128)(2,1)} async-done(((bf16[512,256]{0,1:T(8,128)(2,1)}), bf16[16384,256]{0,1:T(8,128)(2,1)}) %all-gather.2.cloned.1.call-update) | async-done | bytes 8388624 | tf_op jit(solution)/shard_map/all_gather | solution.py:23
  136.5 5.8 %fusion.39 = (bf16[16384,128]{0,1:T(8,128)(2,1)}, bf16[16384,128]{0,1:T(8,128)(2,1)}) fusion(bf16[16384,256]{0,1:T(8,128)(2,1)} %all-gather.2.cloned.1.call-done), kind=kLoop, calls=%fused_computation.62 | loop fusion | bytes 16777216 | tf_op jit(solution)/shard_map/split | solution.py:23
  142.3 6.4 %copy.21 = bf16[16384,128]{1,0:T(8,128)(2,1)} copy(bf16[16384,128]{0,1:T(8,128)(2,1)} %get-tuple-element.495) | data formatting | bytes 8388608 | tf_op jit(solution)/shard_map/while | solution.py:116
  148.8 47.7 %while.21 = (s32[]{:T(128)}, f32[512,1,4]{0,2,1:T(4,128)S(1)}, f32[512,1,4]{0,2,1:T(4,128)S(1)}, f32[512,1,4,128]{0,3,2,1:T(8,128)S(1)}, s32[512]{0:T(512)S(1)},...) while((s32[]{:T(128)}, f32[512,1,4]{0,2,1:T(4,128)S(1)}, ...), condition=%wide.region_8.9_spmd, body=%wide.region_3.8_spmd.sunk | while | flops 1098914816 | bytes 30560620 | solution.py:116
  151.2 8.5 %conditional.2 = ((f32[512,1,4]{0,2,1:T(4,128)S(1)}, f32[512,1,4]{0,2,1:T(4,128)S(1)}, f32[512,1,4,128]{0,3,2,1:T(8,128)S(1)})) conditional(s32[]{:T(128)} %convert_element_type.115, (f32[512,1,4]{0,2,1:T(4,128)S(1)}, f32[512,1,4]{0,2,1:T(4,128)S(1)}, f32[512,1,4,128]{0,3,2,1:T(8,128)S(1)}) %tuple.77, (s32[]{:T(128)}, s32[1024]{0:T(1024)S(1)}, ...), branch_computations={%region_4.4_spmd, %region_5.7_spmd} | conditional | flops 1098914816 | bytes 30556238 | solution.py:101
  151.7 2.5 fusion.2
  154.3 3.5 %fusion.10 = f32[512,1,4,128]{0,3,2,1:T(8,128)S(1)} fusion(f32[1024,512,4]{1,0,2:T(8,128)S(1)} %get-tuple-element.493, f32[512,4]{0,1:T(4,128)S(1)} %bitcast.94, pred[512,1024]{0,1:T(8,128)(4,1)S(1)} %compare_and_fusion, f32[512,1,4,128]{0,3,2,1:T(8,128)S(1)} %get-tuple-element.426, f32[512,4]{0,1:T(4,128)S(1)} %get-tuple-element.490, ...), kind=kOutput, calls=%fused_computation.10 | convolution fusion | flops 545783808 | bytes 11288580 | tf_op jit(solution)/shard_map/while/body/eval_jaxpr/cond/branch_1_fun/qkgs,skd->qkgd/dot_general | solution.py:89
  157.8 1.8 fusion.1
  160.9 0.6 slice.73
  163.3 0.6 slice.73
  165.7 0.6 slice.73
  168.2 0.6 slice.73
  170.6 0.6 slice.73
  173.1 0.6 slice.73
  175.5 0.6 slice.73
  177.9 0.6 slice.73
  180.4 0.6 slice.73
  182.8 0.6 slice.73
  196.7 6.6 %convolution_convert_fusion = bf16[512,4096]{1,0:T(8,128)(2,1)} fusion(bf16[512,512]{0,1:T(8,128)(2,1)S(1)} %bitcast.96, bf16[512,4096]{1,0:T(8,128)(2,1)} %param.16), kind=kOutput, calls=%fused_computation.31 | convolution fusion | flops 2149580800 | bytes 8912896 | tf_op jit(solution)/shard_map/dot_general | solution.py:142
  203.3 121.8 %reduce-scatter.2.cloned.1.call-done = bf16[128,4096]{1,0:T(8,128)(2,1)} async-done(((bf16[512,4096]{1,0:T(8,128)(2,1)}), bf16[128,4096]{1,0:T(8,128)(2,1)}) %reduce-scatter.2.cloned.1.call-update) | async-done | bytes 1048592 | tf_op jit(solution)/shard_map/reduce_scatter | solution.py:141
  325.1 2.4 add_convert_fusion
  (93 shorter events, 15.6 us)
Async XLA Ops:
  6.5 64.7 %copy-start = (bf16[4096,128]{1,0:T(8,128)(2,1)S(1)}, bf16[4096,128]{1,0:T(8,128)(2,1)}, u32[]{:S(2)}) copy-start(bf16[4096,128]{1,0:T(8,128)(2,1)} %param.15) | copy-start | bytes 3145732
  10.3 5.1 %copy-start.6 = (s32[16]{0:T(128)S(1)}, s32[16]{0:T(128)}, u32[]{:S(2)}) copy-start(s32[16]{0:T(128)} %param.17) | copy-start | bytes 196
  10.3 54.0 %all-to-all-start = ((bf16[4,128,4096]{2,1,0:T(8,128)(2,1)}), bf16[4,128,4096]{2,1,0:T(8,128)(2,1)}, u32[]{:S(2)}, u32[]{:S(2)}) async-start(bf16[4,128,4096]{2,1,0:T(8,128)(2,1)} %stack.2), calls=%async_computation | async-start | bytes 8388608 | tf_op jit(solution)/shard_map/all_to_all | solution.py:12
  15.4 52.0 %copy-start.5 = (f32[4096]{0:T(1024)S(1)}, f32[4096]{0:T(1024)}, u32[]{:S(2)}) copy-start(f32[4096]{0:T(1024)} %param.12) | copy-start | bytes 49156
  15.4 121.1 %all-gather.2.cloned.1.call-start = ((), (), s32[]{:S(2)}) async-start(), calls=%async_computation.2 | async-start | bytes 8650752 | tf_op jit(solution)/shard_map/all_gather | solution.py:23
  71.3 1.6 copy-start.4
  75.7 249.4 %reduce-scatter.2.cloned.1.call-start = ((), (), s32[]{:S(2)}) async-start(), calls=%async_computation.3 | async-start | bytes 5242880 | tf_op jit(solution)/shard_map/reduce_scatter | solution.py:141
  82.9 4.0 %copy-start.3 = (bf16[512,4096]{1,0:T(8,128)(2,1)S(1)}, bf16[512,4096]{1,0:T(8,128)(2,1)}, u32[]{:S(2)}) copy-start(bf16[512,4096]{1,0:T(8,128)(2,1)} %copy.24) | copy-start | bytes 12582916
  196.7 130.9 %copy-start.1 = (bf16[4096,128]{1,0:T(8,128)(2,1)S(1)}, bf16[4096,128]{1,0:T(8,128)(2,1)}, u32[]{:S(2)}) copy-start(bf16[4096,128]{1,0:T(8,128)(2,1)} %param.15) | copy-start | bytes 3145732
  203.3 121.8 %copy-start.2 = (bf16[128,4096]{1,0:T(8,128)(2,1)S(1)}, bf16[128,4096]{1,0:T(8,128)(2,1)}, u32[]{:S(2)}) copy-start(bf16[128,4096]{1,0:T(8,128)(2,1)} %param.11) | copy-start | bytes 3145732
Sparse Core Ops, SparseCore 0:
  75.8 60.6 all-gather.1
  203.4 121.6 reduce-scatter.1
